TPU v7x, 256 devices: a whole 4x4x8 slice. The times are simulated.
256 devices in a mesh: px: 4 (over x_lo, core), py: 8 (over y, x_hi), pz: 8 (over z).
Axes of the slice: x: 4 (x_hi: 2, x_lo: 2; x = x_hi * 2 + x_lo), y: 4, z: 8, core: 2. Of those that a mesh axis runs over, the one named last changes fastest.
Arguments:
- control_values: float32 [28, 56, 56, 512], P('px', 'py', 'pz'), may hold values from -6 to 6
- metric_diag: float32 [3, 32, 4096], P(None, 'px', ('py', 'pz')), may hold values from 0.5 to 2
- metric_off: float32 [3, 32, 4096], P(None, 'px', ('py', 'pz')), may hold values from -0.2 to 0.2
- mass_weight: float32 [32, 4096], P('px', ('py', 'pz')), may hold values from 0.5 to 2
- orient: int32 [4, 8, 8, 3], P('px', 'py', 'pz'), may hold values from 0 to 1
Outputs:
- stiffness_out: float32 [28, 56, 56, 512], P('px', 'py', 'pz')
- mass_out: float32 [28, 56, 56, 512], P('px', 'py', 'pz')
All inputs are finite; a program needn't handle non-finite values.
Results may differ from a plain program's by a relative error of at most 0.0003.
Values sent between devices are 32-bit elements; how exact they have to be, the bound alone decides.
A program may use at most 64 MiB of HBM per device.

v0:
```python
import functools
import math

import jax
import jax.numpy as jnp
import numpy as np
from jax import lax
from jax.experimental import pallas as pl
from jax.experimental.pallas import tpu as pltpu
from jax.sharding import PartitionSpec as P

MESH = pl.DeviceIdType.MESH
LANES = 128
F32 = jnp.float32
BF16 = jnp.bfloat16


def spline_tables(elements):
    knot_row = np.concatenate(
        [np.zeros(3), np.arange(elements + 1) * 1.0, np.full(3, float(elements))]
    )
    offsets = np.array([0.5 - 0.5 / math.sqrt(3.0), 0.5 + 0.5 / math.sqrt(3.0)])
    points = (np.arange(elements)[:, None] + offsets[None, :]).reshape(-1)
    intervals = np.repeat(np.arange(elements), 2) + 3
    current = np.zeros((points.size, knot_row.size - 1))
    current[np.arange(points.size), intervals] = 1.0
    previous = current
    for degree in range(1, 4):
        columns = knot_row.size - 1 - degree
        updated = np.zeros((points.size, columns))
        for i in range(columns):
            lower_gap = knot_row[i + degree] - knot_row[i]
            upper_gap = knot_row[i + degree + 1] - knot_row[i + 1]
            if lower_gap > 0:
                updated[:, i] += (points - knot_row[i]) / lower_gap * current[:, i]
            if upper_gap > 0:
                updated[:, i] += (knot_row[i + degree + 1] - points) / upper_gap * current[:, i + 1]
        previous = current
        current = updated
    slopes = np.zeros(current.shape)
    for i in range(current.shape[1]):
        lower_gap = knot_row[i + 3] - knot_row[i]
        upper_gap = knot_row[i + 4] - knot_row[i + 1]
        if lower_gap > 0:
            slopes[:, i] += 3.0 / lower_gap * previous[:, i]
        if upper_gap > 0:
            slopes[:, i] -= 3.0 / upper_gap * previous[:, i + 1]
    return (current.astype(np.float32), slopes.astype(np.float32))


def split(table):
    high = table.astype(np.float32).astype(BF16)
    low = (table.astype(np.float32) - high.astype(np.float32)).astype(BF16)
    return np.asarray(high), np.asarray(low)


def pair_table(first, second):
    wide_first = np.zeros((8, 8))
    wide_first[:, :7] = first
    wide_second = np.zeros((8, 8))
    wide_second[:, :7] = second
    return np.einsum("bj,ck->bcjk", wide_first, wide_second).reshape(64, 64)


def mirrored(table, flip_j, flip_k):
    grid = table.reshape(64, 8, 8).copy()
    if flip_j:
        grid[:, :7] = grid[:, 6::-1]
    if flip_k:
        grid[:, :, :7] = grid[:, :, 6::-1]
    return grid.reshape(64, 64)


def matmul_tables(values, slopes):
    value_value = pair_table(values, values)
    slope_value = pair_table(slopes, values)
    value_slope = pair_table(values, slopes)
    high, low = split(np.concatenate([value_value, slope_value, value_slope]))
    forward = np.concatenate([high, low, high], axis=1)
    back_mixed, back_plain = [], []
    for flips in range(4):
        vv, sv, vs = (
            split(mirrored(t, flips // 2, flips % 2).T) for t in (value_value, slope_value, value_slope)
        )
        none = np.zeros((64, 64), vv[0].dtype)
        mixed = np.concatenate([sv[0], vs[0]], axis=1)
        mixed_low = np.concatenate([sv[1], vs[1], none, none], axis=1)
        back_mixed.append(np.concatenate([np.concatenate([mixed, mixed], axis=1), mixed_low]))
        back_plain.append(
            np.concatenate(
                [
                    np.concatenate([vv[0], vv[0], none, none], axis=1),
                    np.concatenate([vv[1], none, none, none], axis=1),
                    np.concatenate([none, none, vv[0], vv[0]], axis=1),
                    np.concatenate([none, none, vv[1], none], axis=1),
                ]
            )
        )
    return forward, np.stack(back_mixed), np.stack(back_plain)


def halves(x):
    high = x.astype(BF16)
    low = (x - high.astype(F32)).astype(BF16)
    return high, low


def mac(terms):
    total = None
    for coefficient, x in terms:
        part = x * float(coefficient)
        total = part if total is None else total + part
    return total


def kernel(
    values, slopes, tiles,
    control, diag, off, weight, orient, forward, mixed, plain,
    stiff_out, mass_out,
    ubuf, gbuf, planes, metric, scales, staged,
    xrecv, yrecv, zsend, zrecv,
    load_sem, out_sem, send_sem, recv_sem,
):
    px, py, pz = (lax.axis_index(a) for a in ("px", "py", "pz"))
    nx, ny, nz = (lax.axis_size(a) for a in ("px", "py", "pz"))
    x_up, x_down = lax.rem(px + 1, nx), lax.rem(px + nx - 1, nx)
    y_up, y_down = lax.rem(py + 1, ny), lax.rem(py + ny - 1, ny)
    z_up, z_down = lax.rem(pz + 1, nz), lax.rem(pz + nz - 1, nz)
    x_mirror = nx - 1 - px
    odd = lax.rem(px, 2)
    rim, first = 6 * odd, 1 - odd

    barrier = pltpu.get_barrier_semaphore()
    for device in (
        (x_up, py, pz), (x_down, py, pz),
        (px, y_up, pz), (px, y_down, pz), (x_mirror, y_up, pz), (x_mirror, y_down, pz),
        (px, py, z_up), (px, py, z_down),
    ):
        pl.semaphore_signal(barrier, inc=1, device_id=device, device_id_type=MESH)

    def load(t):
        return pltpu.make_async_copy(
            control.at[:, :, :, pl.ds(pl.multiple_of(t * LANES, LANES), LANES)],
            ubuf.at[t, :, :, pl.ds(0, 7), :],
            load_sem.at[t],
        )

    for t in range(tiles):
        load(t).start()
    pad = jnp.zeros((7, 7, 1, LANES), F32)
    for t in range(tiles):
        ubuf[t, :, :, pl.ds(7, 1), :] = pad

    flip_i, flip_j, flip_k = (orient[0, 0, 0, d] for d in range(3))
    variant = 2 * flip_j + flip_k

    scales[pl.ds(0, 24), pl.ds(0, 64)] = diag[...].reshape(24, 64)
    scales[pl.ds(24, 24), pl.ds(0, 64)] = off[...].reshape(24, 64)
    scales[pl.ds(48, 8), pl.ds(0, 64)] = weight[...]
    turned = scales[...].T
    for m in range(56):
        metric[m] = jnp.broadcast_to(turned[:64, m : m + 1], (64, LANES))

    def compute(t):
        load(t).wait()
        forward_table = forward[...]
        mixed_table = mixed[variant]
        plain_table = plain[variant]
        nothing = jnp.zeros((8, LANES), F32)
        for e in range(4):
            source = [ubuf[t, i].reshape(56, LANES) for i in range(e, e + 4)]
            value_cat, slope_cat = [], []
            for a in (2 * e, 2 * e + 1):
                for table, cat in ((values, value_cat), (slopes, slope_cat)):
                    x = mac([(table[a, e + n], source[n]) for n in range(4)])
                    high, low = halves(jnp.concatenate([x, nothing], axis=0))
                    cat.append(jnp.concatenate([high, high, low], axis=0))
            at_values = jnp.dot(
                forward_table, jnp.concatenate(value_cat, axis=1), preferred_element_type=F32
            )
            at_slopes = jnp.dot(
                forward_table[:64], jnp.concatenate(slope_cat, axis=1), preferred_element_type=F32
            )
            mixed_in, plain_in = [], []
            for n, a in enumerate((2 * e, 2 * e + 1)):
                lanes = slice(n * LANES, (n + 1) * LANES)
                p, g2, g3 = (at_values[64 * r : 64 * r + 64, lanes] for r in range(3))
                g1 = at_slopes[:, lanes]
                d0, d1, d2, o0, o1, o2, w = (metric[8 * s + a] for s in range(7))
                f1 = d0 * g1 + o0 * g2 + o1 * g3
                f2 = o0 * g1 + d1 * g2 + o2 * g3
                f3 = o1 * g1 + o2 * g2 + d2 * g3
                f1h, f1l = halves(f1)
                f2h, f2l = halves(f2)
                f3h, f3l = halves(f3)
                mh, ml = halves(w * p)
                mixed_in.append(jnp.concatenate([f2h, f3h, f2l, f3l], axis=0))
                plain_in.append(jnp.concatenate([f1h, f1l, mh, ml], axis=0))
            mixed_back = jnp.dot(
                mixed_table, jnp.concatenate(mixed_in, axis=1), preferred_element_type=F32
            )
            plain_back = jnp.dot(
                plain_table, jnp.concatenate(plain_in, axis=1), preferred_element_type=F32
            )
            terms = []
            for n in range(2):
                lanes = slice(n * LANES, (n + 1) * LANES)
                terms.append(
                    (
                        plain_back[0:56, lanes] + plain_back[64:120, lanes],
                        mixed_back[0:56, lanes] + mixed_back[64:120, lanes],
                        plain_back[128:184, lanes] + plain_back[192:248, lanes],
                    )
                )
            for i in range(e, e + 4):
                stiff = mac(
                    [(slopes[2 * e + n, i], terms[n][0]) for n in range(2)]
                    + [(values[2 * e + n, i], terms[n][1]) for n in range(2)]
                )
                mass = mac([(values[2 * e + n, i], terms[n][2]) for n in range(2)])
                if e > 0 and i < e + 3:
                    stiff = stiff + planes[0, i]
                    mass = mass + planes[1, i]
                planes[0, i] = stiff
                planes[1, i] = mass
        for o in range(2):
            for i in range(7):
                gbuf[o, t, i] = planes[o, i + flip_i * (6 - 2 * i)].reshape(7, 8, LANES)

    def remote(t, which, src, dst, device):
        return pltpu.make_async_remote_copy(
            src_ref=src, dst_ref=dst, send_sem=send_sem.at[t, which], recv_sem=recv_sem.at[t, which],
            device_id=device, device_id_type=MESH,
        )

    rows = pl.ds(0, 7)

    def x_copies(t):
        return [
            remote(t, 0, gbuf.at[:, t, 6, :, rows, :], xrecv.at[t, 0, :, :, rows, :], (x_up, py, pz)),
            remote(t, 1, gbuf.at[:, t, 0, :, rows, :], xrecv.at[t, 1, :, :, rows, :], (x_down, py, pz)),
        ]

    def y_copies(t):
        inner = pl.ds(first, 6)
        return [
            remote(t, 2, gbuf.at[:, t, inner, 6, rows, :], yrecv.at[t, 0, :, inner, rows, :], (px, y_up, pz)),
            remote(t, 3, gbuf.at[:, t, inner, 0, rows, :], yrecv.at[t, 1, :, inner, rows, :], (px, y_down, pz)),
            remote(t, 4, gbuf.at[:, t, rim, 6, rows, :], yrecv.at[t, 0, :, 6 - rim, rows, :], (x_mirror, y_up, pz)),
            remote(t, 5, gbuf.at[:, t, rim, 0, rows, :], yrecv.at[t, 1, :, 6 - rim, rows, :], (x_mirror, y_down, pz)),
        ]

    def z_copies(t):
        return [
            remote(t, 6, zsend.at[t, 1], zrecv.at[t, 0], (px, py, z_up)),
            remote(t, 7, zsend.at[t, 0], zrecv.at[t, 1], (px, py, z_down)),
        ]

    def start(copies):
        for c in copies:
            c.start()

    def wait(copies):
        for c in copies:
            c.wait()

    def fold_x(t):
        for side in range(2):
            for o in range(2):
                gbuf[o, t, 6 * side, :, rows, :] = (
                    gbuf[o, t, 6 * side, :, rows, :] + xrecv[t, side, o, :, rows, :]
                )

    def fold_y(t):
        for side in range(2):
            for o in range(2):
                gbuf[o, t, :, 6 * side, rows, :] = (
                    gbuf[o, t, :, 6 * side, rows, :] + yrecv[t, side, o, :, rows, :]
                )

    def take_z(t):
        for side in range(2):
            for o in range(2):
                for i in range(7):
                    zsend[t, side, o, i] = gbuf[o, t, i, :, 6 * side, :]

    def fold_z(t):
        for side in range(2):
            for o in range(2):
                for i in range(7):
                    gbuf[o, t, i, :, 6 * side, :] = gbuf[o, t, i, :, 6 * side, :] + zrecv[t, side, o, i]

    sublane = lax.broadcasted_iota(jnp.int32, (8, LANES), 0)
    turned_rows = jnp.where(sublane < 7, 6 - sublane, sublane)
    pick = sublane + flip_k * (turned_rows - sublane)

    def out_copies(t):
        lanes = pl.ds(pl.multiple_of(t * LANES, LANES), LANES)
        return [
            pltpu.make_async_copy(staged.at[o, t, :, :, rows, :], out.at[:, :, :, lanes], out_sem.at[o, t])
            for o, out in enumerate((stiff_out, mass_out))
        ]

    def finish(t):
        for o in range(2):
            for i in range(7):
                for j in range(7):
                    tile = gbuf[o, t, i + flip_i * (6 - 2 * i), j + flip_j * (6 - 2 * j)]
                    staged[o, t, i, j] = jnp.take_along_axis(tile, pick, axis=0)
        start(out_copies(t))

    def step(s, carry):
        @pl.when(s < tiles)
        def _():
            compute(s)

            @pl.when(s == 0)
            def _():
                pl.semaphore_wait(barrier, 8)

            start(x_copies(s))

        @pl.when(jnp.logical_and(s >= 1, s < tiles + 1))
        def _():
            wait(x_copies(s - 1))
            fold_x(s - 1)
            start(y_copies(s - 1))

        @pl.when(jnp.logical_and(s >= 2, s < tiles + 2))
        def _():
            wait(y_copies(s - 2))
            fold_y(s - 2)
            take_z(s - 2)
            start(z_copies(s - 2))

        @pl.when(s >= 3)
        def _():
            wait(z_copies(s - 3))
            fold_z(s - 3)
            finish(s - 3)

        return carry

    lax.fori_loop(0, tiles + 3, step, 0)
    for t in range(tiles):
        wait(out_copies(t))


def per_device(control_values, metric_diag, metric_off, mass_weight, orient):
    values, slopes = spline_tables(4)
    tiles = control_values.shape[-1] // LANES
    forward, mixed, plain = (jnp.asarray(t) for t in matmul_tables(values, slopes))
    shape = jax.ShapeDtypeStruct(control_values.shape, F32)
    in_vmem = pl.BlockSpec(memory_space=pltpu.VMEM)
    anywhere = pl.BlockSpec(memory_space=pl.ANY)
    return pl.pallas_call(
        functools.partial(kernel, values, slopes, tiles),
        out_shape=(shape, shape),
        in_specs=[anywhere, in_vmem, in_vmem, in_vmem, pl.BlockSpec(memory_space=pltpu.SMEM)] + [in_vmem] * 3,
        out_specs=(anywhere, anywhere),
        scratch_shapes=[
            pltpu.VMEM((tiles, 7, 7, 8, LANES), F32),
            pltpu.VMEM((2, tiles, 7, 7, 8, LANES), F32),
            pltpu.VMEM((2, 7, 56, LANES), F32),
            pltpu.VMEM((56, 64, LANES), F32),
            pltpu.VMEM((128, 128), F32),
            pltpu.VMEM((2, tiles, 7, 7, 8, LANES), F32),
            pltpu.VMEM((tiles, 2, 2, 7, 8, LANES), F32),
            pltpu.VMEM((tiles, 2, 2, 7, 8, LANES), F32),
            pltpu.VMEM((tiles, 2, 2, 7, 7, LANES), F32),
            pltpu.VMEM((tiles, 2, 2, 7, 7, LANES), F32),
            pltpu.SemaphoreType.DMA((tiles,)),
            pltpu.SemaphoreType.DMA((2, tiles)),
            pltpu.SemaphoreType.DMA((tiles, 8)),
            pltpu.SemaphoreType.DMA((tiles, 8)),
        ],
        compiler_params=pltpu.CompilerParams(
            collective_id=0, has_side_effects=True, vmem_limit_bytes=40 * 1024 * 1024
        ),
        name="apply",
    )(control_values, metric_diag, metric_off, mass_weight, orient, forward, mixed, plain)


def solution(mesh):
    in_specs = (
        P("px", "py", "pz", None),
        P(None, "px", ("py", "pz")),
        P(None, "px", ("py", "pz")),
        P("px", ("py", "pz")),
        P("px", "py", "pz", None),
    )
    out_specs = (P("px", "py", "pz", None), P("px", "py", "pz", None))
    return jax.shard_map(
        per_device, mesh=mesh, in_specs=in_specs, out_specs=out_specs, check_vma=False
    )
```

profile of v0, /device:TPU:1, one launch (start us, length us, event | category | flops | bytes accessed | tf_op | source)
XLA Modules:
  0.0 43.3 jit_solution(3008286922812897384)
XLA Ops:
  0.6 0.0 copy-start
  0.6 1.1 %copy-done = f32[7,7,7,512]{3,2,1,0:T(8,128)S(1)} copy-done((f32[7,7,7,512]{3,2,1,0:T(8,128)S(1)}, f32[7,7,7,512]{3,2,1,0:T(8,128)}, u32[]{:S(2)}) %copy-start) | copy-done | bytes 702488
  1.8 0.0 copy-start.1
  1.8 1.0 %copy-done.1 = bf16[4,256,256]{2,1,0:T(8,128)(2,1)S(1)} copy-done((bf16[4,256,256]{2,1,0:T(8,128)(2,1)S(1)}, bf16[4,256,256]{2,1,0:T(8,128)(2,1)}, u32[]{:S(2)}) %copy-start.1) | copy-done | bytes 524312
  2.8 0.0 copy-start.2
  2.8 0.9 %copy-done.2 = bf16[4,128,256]{2,1,0:T(8,128)(2,1)S(1)} copy-done((bf16[4,128,256]{2,1,0:T(8,128)(2,1)S(1)}, bf16[4,128,256]{2,1,0:T(8,128)(2,1)}, u32[]{:S(2)}) %copy-start.2) | copy-done | bytes 262168
  3.8 0.0 copy-start.3
  3.8 0.9 %copy-done.3 = bf16[192,192]{1,0:T(8,128)(2,1)S(1)} copy-done((bf16[192,192]{1,0:T(8,128)(2,1)S(1)}, bf16[192,192]{1,0:T(8,128)(2,1)}, u32[]{:S(2)}) %copy-start.3) | copy-done | bytes 73752
  4.7 0.0 copy-start.4
  4.7 0.7 %copy-done.4 = f32[3,8,64]{2,1,0:T(8,128)S(1)} copy-done((f32[3,8,64]{2,1,0:T(8,128)S(1)}, f32[3,8,64]{2,1,0:T(8,128)}, u32[]{:S(2)}) %copy-start.4) | copy-done | bytes 6168
  5.4 0.0 copy-start.5
  5.4 0.7 %copy-done.5 = f32[3,8,64]{2,1,0:T(8,128)S(1)} copy-done((f32[3,8,64]{2,1,0:T(8,128)S(1)}, f32[3,8,64]{2,1,0:T(8,128)}, u32[]{:S(2)}) %copy-start.5) | copy-done | bytes 6168
  6.1 0.0 copy-start.6
  6.1 0.7 %copy-done.6 = f32[8,64]{1,0:T(8,128)S(1)} copy-done((f32[8,64]{1,0:T(8,128)S(1)}, f32[8,64]{1,0:T(8,128)}, u32[]{:S(2)}) %copy-start.6) | copy-done | bytes 2072
  6.8 0.0 copy-start.7
  6.8 0.7 %copy-done.7 = s32[1,1,1,3]{3,2,1,0:T(1,128)S(1)} copy-done((s32[1,1,1,3]{3,2,1,0:T(1,128)S(1)}, s32[1,1,1,3]{3,2,1,0:T(1,128)}, u32[]{:S(2)}) %copy-start.7) | copy-done | bytes 36
  7.4 34.1 %apply.1 = (f32[7,7,7,512]{3,2,1,0:T(8,128)S(1)}, f32[7,7,7,512]{3,2,1,0:T(8,128)S(1)}) custom-call(f32[7,7,7,512]{3,2,1,0:T(8,128)S(1)} %copy-done, f32[3,8,64]{2,1,0:T(8,128)S(1)} %copy-done.4, f32[3,8,64]{2,1,0:T(8,128)S(1)} %copy-done.5, f32[8,64]{1,0:T(8,128)S(1)} %copy-done.6, s32[1,1,1,3]{3,2,1,0:T(1,128)S(1)} %copy-done.7, ...), custom_call_target="tpu_custom_call" | custom-call | tf_op jit(solution)/shard_map/apply/pallas_call | solution.py:356
  41.5 0.9 %copy.12 = f32[7,7,7,512]{3,2,1,0:T(8,128)} copy(f32[7,7,7,512]{3,2,1,0:T(8,128)S(1)} %get-tuple-element.4) | data formatting | bytes 1404928
  42.4 0.9 %copy.13 = f32[7,7,7,512]{3,2,1,0:T(8,128)} copy(f32[7,7,7,512]{3,2,1,0:T(8,128)S(1)} %get-tuple-element.5) | data formatting | bytes 1404928
Async XLA Ops:
  0.6 1.1 %copy-start = (f32[7,7,7,512]{3,2,1,0:T(8,128)S(1)}, f32[7,7,7,512]{3,2,1,0:T(8,128)}, u32[]{:S(2)}) copy-start(f32[7,7,7,512]{3,2,1,0:T(8,128)} %control.1) | copy-start | bytes 2107396
  1.8 1.0 %copy-start.1 = (bf16[4,256,256]{2,1,0:T(8,128)(2,1)S(1)}, bf16[4,256,256]{2,1,0:T(8,128)(2,1)}, u32[]{:S(2)}) copy-start(bf16[4,256,256]{2,1,0:T(8,128)(2,1)} %constant.8.clone.plain) | copy-start | bytes 1572868
  2.8 0.9 %copy-start.2 = (bf16[4,128,256]{2,1,0:T(8,128)(2,1)S(1)}, bf16[4,128,256]{2,1,0:T(8,128)(2,1)}, u32[]{:S(2)}) copy-start(bf16[4,128,256]{2,1,0:T(8,128)(2,1)} %constant.7.clone.mixed) | copy-start | bytes 786436
  3.8 0.9 %copy-start.3 = (bf16[192,192]{1,0:T(8,128)(2,1)S(1)}, bf16[192,192]{1,0:T(8,128)(2,1)}, u32[]{:S(2)}) copy-start(bf16[192,192]{1,0:T(8,128)(2,1)} %constant.6.clone.forward) | copy-start | bytes 221188
  4.7 0.7 %copy-start.4 = (f32[3,8,64]{2,1,0:T(8,128)S(1)}, f32[3,8,64]{2,1,0:T(8,128)}, u32[]{:S(2)}) copy-start(f32[3,8,64]{2,1,0:T(8,128)} %diag.1) | copy-start | bytes 18436
  5.4 0.7 %copy-start.5 = (f32[3,8,64]{2,1,0:T(8,128)S(1)}, f32[3,8,64]{2,1,0:T(8,128)}, u32[]{:S(2)}) copy-start(f32[3,8,64]{2,1,0:T(8,128)} %off.1) | copy-start | bytes 18436
  6.1 0.7 %copy-start.6 = (f32[8,64]{1,0:T(8,128)S(1)}, f32[8,64]{1,0:T(8,128)}, u32[]{:S(2)}) copy-start(f32[8,64]{1,0:T(8,128)} %weight.1) | copy-start | bytes 6148
  6.8 0.7 %copy-start.7 = (s32[1,1,1,3]{3,2,1,0:T(1,128)S(1)}, s32[1,1,1,3]{3,2,1,0:T(1,128)}, u32[]{:S(2)}) copy-start(s32[1,1,1,3]{3,2,1,0:T(1,128)} %orient.1) | copy-start | bytes 40
where the time goes:
time: 43.6 us; the launch traced here: 43.3 us
  Pallas kernels  34.1 us (78%)
  local copies, waits for them, and re-layouts  8.54 us (20%)
  between operations  0.66 us (2%)
    pallas_call x1, Pallas kernels, per_device(): pl.pallas_call(functools.partial(kernel, values, slopes, tiles), out_shap...  34.1 us
    unnamed x18, local copies, waits for them, and re-layouts  8.54 us

commit v1 on v0

--- a/solution.py
+++ b/solution.py
@@ -115,11 +115,13 @@
 
 def kernel(
     values, slopes, tiles,
-    control, diag, off, weight, orient, forward, mixed, plain,
+    control, diag_in, off_in, weight_in, orient_in, forward_in, mixed_in_hbm, plain_in_hbm,
     stiff_out, mass_out,
-    ubuf, gbuf, planes, metric, scales, staged,
-    xrecv, yrecv, zsend, zrecv,
-    load_sem, out_sem, send_sem, recv_sem,
+    diag, off, weight, orient, forward, mixed, plain,
+    ubuf, gbuf, planes, metric, scales,
+    xrecv, ysend_inner, yrecv_inner, ysend_ends, yrecv_ends, yrecv_sides,
+    zsend_inner, zrecv_inner, zsend_sides, zrecv_sides,
+    load_sem, small_sem, send_sem, recv_sem,
 ):
     px, py, pz = (lax.axis_index(a) for a in ("px", "py", "pz"))
     nx, ny, nz = (lax.axis_size(a) for a in ("px", "py", "pz"))
@@ -128,7 +130,7 @@
     z_up, z_down = lax.rem(pz + 1, nz), lax.rem(pz + nz - 1, nz)
     x_mirror = nx - 1 - px
     odd = lax.rem(px, 2)
-    rim, first = 6 * odd, 1 - odd
+    rim = 6 * odd
 
     barrier = pltpu.get_barrier_semaphore()
     for device in (
@@ -145,12 +147,28 @@
             load_sem.at[t],
         )
 
-    for t in range(tiles):
+    small = [
+        pltpu.make_async_copy(src, dst, small_sem.at[n])
+        for n, (src, dst) in enumerate(
+            (
+                (orient_in, orient), (diag_in, diag), (off_in, off), (weight_in, weight),
+                (forward_in, forward), (mixed_in_hbm, mixed), (plain_in_hbm, plain),
+            )
+        )
+    ]
+    for c in small[:4]:
+        c.start()
+    load(0).start()
+    for c in small[4:]:
+        c.start()
+    for t in range(1, tiles):
         load(t).start()
     pad = jnp.zeros((7, 7, 1, LANES), F32)
     for t in range(tiles):
         ubuf[t, :, :, pl.ds(7, 1), :] = pad
 
+    for c in small[:4]:
+        c.wait()
     flip_i, flip_j, flip_k = (orient[0, 0, 0, d] for d in range(3))
     variant = 2 * flip_j + flip_k
 
@@ -161,13 +179,16 @@
     for m in range(56):
         metric[m] = jnp.broadcast_to(turned[:64, m : m + 1], (64, LANES))
 
+    for c in small[4:]:
+        c.wait()
+
     def compute(t):
         load(t).wait()
         forward_table = forward[...]
         mixed_table = mixed[variant]
         plain_table = plain[variant]
         nothing = jnp.zeros((8, LANES), F32)
-        for e in range(4):
+        def ahead(e):
             source = [ubuf[t, i].reshape(56, LANES) for i in range(e, e + 4)]
             value_cat, slope_cat = [], []
             for a in (2 * e, 2 * e + 1):
@@ -181,6 +202,9 @@
             at_slopes = jnp.dot(
                 forward_table[:64], jnp.concatenate(slope_cat, axis=1), preferred_element_type=F32
             )
+            return at_values, at_slopes
+
+        def back(e, at_values, at_slopes):
             mixed_in, plain_in = [], []
             for n, a in enumerate((2 * e, 2 * e + 1)):
                 lanes = slice(n * LANES, (n + 1) * LANES)
@@ -202,6 +226,9 @@
             plain_back = jnp.dot(
                 plain_table, jnp.concatenate(plain_in, axis=1), preferred_element_type=F32
             )
+            return mixed_back, plain_back
+
+        def gather(e, mixed_back, plain_back):
             terms = []
             for n in range(2):
                 lanes = slice(n * LANES, (n + 1) * LANES)
@@ -223,6 +250,16 @@
                     mass = mass + planes[1, i]
                 planes[0, i] = stiff
                 planes[1, i] = mass
+
+        up = {0: ahead(0), 1: ahead(1)}
+        down = {}
+        for e in range(4):
+            down[e] = back(e, *up.pop(e))
+            if e + 2 < 4:
+                up[e + 2] = ahead(e + 2)
+            if e >= 1:
+                gather(e - 1, *down.pop(e - 1))
+        gather(3, *down.pop(3))
         for o in range(2):
             for i in range(7):
                 gbuf[o, t, i] = planes[o, i + flip_i * (6 - 2 * i)].reshape(7, 8, LANES)
@@ -241,20 +278,39 @@
             remote(t, 1, gbuf.at[:, t, 0, :, rows, :], xrecv.at[t, 1, :, :, rows, :], (x_down, py, pz)),
         ]
 
-    def y_copies(t):
-        inner = pl.ds(first, 6)
+    def y_pair(t, which, sent, received):
         return [
-            remote(t, 2, gbuf.at[:, t, inner, 6, rows, :], yrecv.at[t, 0, :, inner, rows, :], (px, y_up, pz)),
-            remote(t, 3, gbuf.at[:, t, inner, 0, rows, :], yrecv.at[t, 1, :, inner, rows, :], (px, y_down, pz)),
-            remote(t, 4, gbuf.at[:, t, rim, 6, rows, :], yrecv.at[t, 0, :, 6 - rim, rows, :], (x_mirror, y_up, pz)),
-            remote(t, 5, gbuf.at[:, t, rim, 0, rows, :], yrecv.at[t, 1, :, 6 - rim, rows, :], (x_mirror, y_down, pz)),
+            remote(t, which, sent.at[t, 1], received.at[t, 0], (px, y_up, pz)),
+            remote(t, which + 1, sent.at[t, 0], received.at[t, 1], (px, y_down, pz)),
         ]
 
-    def z_copies(t):
+    def y_inner(t):
+        return y_pair(t, 2, ysend_inner, yrecv_inner)
+
+    def y_ends(t):
+        return y_pair(t, 4, ysend_ends, yrecv_ends)
+
+    def y_sides(t):
+        near = 6 - rim
+        there = 1 - odd
         return [
-            remote(t, 6, zsend.at[t, 1], zrecv.at[t, 0], (px, py, z_up)),
-            remote(t, 7, zsend.at[t, 0], zrecv.at[t, 1], (px, py, z_down)),
+            remote(t, 6, gbuf.at[:, t, near, 6, rows, :], yrecv_sides.at[t, 0, there, :, rows, :], (px, y_up, pz)),
+            remote(t, 7, gbuf.at[:, t, near, 0, rows, :], yrecv_sides.at[t, 1, there, :, rows, :], (px, y_down, pz)),
+            remote(t, 8, gbuf.at[:, t, rim, 6, rows, :], yrecv_sides.at[t, 0, there, :, rows, :], (x_mirror, y_up, pz)),
+            remote(t, 9, gbuf.at[:, t, rim, 0, rows, :], yrecv_sides.at[t, 1, there, :, rows, :], (x_mirror, y_down, pz)),
         ]
+
+    def z_pair(t, which, sent, received):
+        return [
+            remote(t, which, sent.at[t, 1], received.at[t, 0], (px, py, z_up)),
+            remote(t, which + 1, sent.at[t, 0], received.at[t, 1], (px, py, z_down)),
+        ]
+
+    def z_inner(t):
+        return z_pair(t, 10, zsend_inner, zrecv_inner)
+
+    def z_sides(t):
+        return z_pair(t, 12, zsend_sides, zrecv_sides)
 
     def start(copies):
         for c in copies:
@@ -271,79 +327,114 @@
                     gbuf[o, t, 6 * side, :, rows, :] + xrecv[t, side, o, :, rows, :]
                 )
 
+    inner_rows = [(i, i - 1) for i in range(1, 6)]
+    side_rows = [(6 * n, n) for n in range(2)]
+
+    def take_z(t, sent, where):
+        for side in range(2):
+            for o in range(2):
+                for i, n in where:
+                    sent[t, side, o, n] = gbuf[o, t, i, :, 6 * side, :]
+
+    def fold_z(t, received, where):
+        for side in range(2):
+            for o in range(2):
+                for i, n in where:
+                    gbuf[o, t, i, :, 6 * side, :] = gbuf[o, t, i, :, 6 * side, :] + received[t, side, o, n]
+
+    mid = pl.ds(1, 5)
+
+    def take_y_inner(t):
+        for side in range(2):
+            for o in range(2):
+                ysend_inner[t, side, o] = gbuf[o, t, mid, 6 * side, mid, :]
+
+    def take_y_ends(t):
+        for side in range(2):
+            for o in range(2):
+                for n in range(2):
+                    ysend_ends[t, side, o, n] = gbuf[o, t, mid, 6 * side, 6 * n, :]
+
     def fold_y(t):
         for side in range(2):
             for o in range(2):
-                gbuf[o, t, :, 6 * side, rows, :] = (
-                    gbuf[o, t, :, 6 * side, rows, :] + yrecv[t, side, o, :, rows, :]
-                )
-
-    def take_z(t):
-        for side in range(2):
-            for o in range(2):
-                for i in range(7):
-                    zsend[t, side, o, i] = gbuf[o, t, i, :, 6 * side, :]
-
-    def fold_z(t):
-        for side in range(2):
-            for o in range(2):
-                for i in range(7):
-                    gbuf[o, t, i, :, 6 * side, :] = gbuf[o, t, i, :, 6 * side, :] + zrecv[t, side, o, i]
+                j = 6 * side
+                gbuf[o, t, mid, j, mid, :] = gbuf[o, t, mid, j, mid, :] + yrecv_inner[t, side, o]
+                for n in range(2):
+                    gbuf[o, t, mid, j, 6 * n, :] = gbuf[o, t, mid, j, 6 * n, :] + yrecv_ends[t, side, o, n]
+                    gbuf[o, t, 6 * n, j, rows, :] = gbuf[o, t, 6 * n, j, rows, :] + yrecv_sides[t, side, n, o, rows, :]
 
     sublane = lax.broadcasted_iota(jnp.int32, (8, LANES), 0)
     turned_rows = jnp.where(sublane < 7, 6 - sublane, sublane)
     pick = sublane + flip_k * (turned_rows - sublane)
 
-    def out_copies(t):
+    def finish(t):
         lanes = pl.ds(pl.multiple_of(t * LANES, LANES), LANES)
-        return [
-            pltpu.make_async_copy(staged.at[o, t, :, :, rows, :], out.at[:, :, :, lanes], out_sem.at[o, t])
-            for o, out in enumerate((stiff_out, mass_out))
-        ]
-
-    def finish(t):
-        for o in range(2):
+        for o, out in enumerate((stiff_out, mass_out)):
             for i in range(7):
                 for j in range(7):
                     tile = gbuf[o, t, i + flip_i * (6 - 2 * i), j + flip_j * (6 - 2 * j)]
-                    staged[o, t, i, j] = jnp.take_along_axis(tile, pick, axis=0)
-        start(out_copies(t))
-
-    def step(s, carry):
-        @pl.when(s < tiles)
+                    out[i, j, :, lanes] = jnp.take_along_axis(tile, pick, axis=0)[:7]
+
+    def produce(t, carry):
+        compute(t)
+
+        @pl.when(t == 0)
         def _():
-            compute(s)
-
-            @pl.when(s == 0)
-            def _():
-                pl.semaphore_wait(barrier, 8)
-
-            start(x_copies(s))
-
-        @pl.when(jnp.logical_and(s >= 1, s < tiles + 1))
+            pl.semaphore_wait(barrier, 8)
+
+        start(x_copies(t))
+        take_z(t, zsend_inner, inner_rows)
+        start(z_inner(t))
+        take_y_inner(t)
+
+        @pl.when(t >= 1)
         def _():
-            wait(x_copies(s - 1))
-            fold_x(s - 1)
-            start(y_copies(s - 1))
-
-        @pl.when(jnp.logical_and(s >= 2, s < tiles + 2))
-        def _():
-            wait(y_copies(s - 2))
-            fold_y(s - 2)
-            take_z(s - 2)
-            start(z_copies(s - 2))
-
-        @pl.when(s >= 3)
-        def _():
-            wait(z_copies(s - 3))
-            fold_z(s - 3)
-            finish(s - 3)
+            start(y_inner(t - 1))
 
         return carry
 
-    lax.fori_loop(0, tiles + 3, step, 0)
-    for t in range(tiles):
-        wait(out_copies(t))
+    def after_x(t, carry):
+        wait(x_copies(t))
+        fold_x(t)
+        take_z(t, zsend_sides, side_rows)
+        start(z_sides(t))
+        return carry
+
+    def after_z(t, carry):
+        wait(z_inner(t))
+        fold_z(t, zrecv_inner, inner_rows)
+        take_y_ends(t)
+        start(y_ends(t))
+        wait(z_sides(t))
+        fold_z(t, zrecv_sides, side_rows)
+        start(y_sides(t))
+        return carry
+
+    def after_y(t, carry):
+        wait(y_inner(t))
+        wait(y_ends(t))
+        wait(y_sides(t))
+        fold_y(t)
+        finish(t)
+        return carry
+
+    lax.fori_loop(0, tiles, produce, 0)
+    start(y_inner(tiles - 1))
+    for stage in (after_x, after_z, after_y):
+        lax.fori_loop(0, tiles, stage, 0)
+
+
+def put(stiff, mass, stiff_out, mass_out, sem):
+    copies = [
+        pltpu.make_async_copy(source.at[i], target.at[i], sem.at[n, i])
+        for i in range(7)
+        for n, (source, target) in enumerate(((stiff, stiff_out), (mass, mass_out)))
+    ]
+    for c in copies:
+        c.start()
+    for c in copies:
+        c.wait()
 
 
 def per_device(control_values, metric_diag, metric_off, mass_weight, orient):
@@ -352,33 +443,59 @@
     forward, mixed, plain = (jnp.asarray(t) for t in matmul_tables(values, slopes))
     shape = jax.ShapeDtypeStruct(control_values.shape, F32)
     in_vmem = pl.BlockSpec(memory_space=pltpu.VMEM)
-    anywhere = pl.BlockSpec(memory_space=pl.ANY)
-    return pl.pallas_call(
+    in_hbm = pl.BlockSpec(memory_space=pltpu.HBM)
+    results = pl.pallas_call(
         functools.partial(kernel, values, slopes, tiles),
-        out_shape=(shape, shape),
-        in_specs=[anywhere, in_vmem, in_vmem, in_vmem, pl.BlockSpec(memory_space=pltpu.SMEM)] + [in_vmem] * 3,
-        out_specs=(anywhere, anywhere),
+        out_shape=(pltpu.VMEM(control_values.shape, F32),) * 2,
+        in_specs=[in_hbm] * 8,
+        out_specs=(in_vmem, in_vmem),
         scratch_shapes=[
+            pltpu.VMEM(metric_diag.shape, F32),
+            pltpu.VMEM(metric_off.shape, F32),
+            pltpu.VMEM(mass_weight.shape, F32),
+            pltpu.SMEM(orient.shape, jnp.int32),
+            pltpu.VMEM(forward.shape, BF16),
+            pltpu.VMEM(mixed.shape, BF16),
+            pltpu.VMEM(plain.shape, BF16),
             pltpu.VMEM((tiles, 7, 7, 8, LANES), F32),
             pltpu.VMEM((2, tiles, 7, 7, 8, LANES), F32),
             pltpu.VMEM((2, 7, 56, LANES), F32),
             pltpu.VMEM((56, 64, LANES), F32),
             pltpu.VMEM((128, 128), F32),
-            pltpu.VMEM((2, tiles, 7, 7, 8, LANES), F32),
             pltpu.VMEM((tiles, 2, 2, 7, 8, LANES), F32),
-            pltpu.VMEM((tiles, 2, 2, 7, 8, LANES), F32),
-            pltpu.VMEM((tiles, 2, 2, 7, 7, LANES), F32),
-            pltpu.VMEM((tiles, 2, 2, 7, 7, LANES), F32),
+            pltpu.VMEM((tiles, 2, 2, 5, 5, LANES), F32),
+            pltpu.VMEM((tiles, 2, 2, 5, 5, LANES), F32),
+            pltpu.VMEM((tiles, 2, 2, 2, 5, LANES), F32),
+            pltpu.VMEM((tiles, 2, 2, 2, 5, LANES), F32),
+            pltpu.VMEM((tiles, 2, 2, 2, 8, LANES), F32),
+            pltpu.VMEM((tiles, 2, 2, 5, 7, LANES), F32),
+            pltpu.VMEM((tiles, 2, 2, 5, 7, LANES), F32),
+            pltpu.VMEM((tiles, 2, 2, 2, 7, LANES), F32),
+            pltpu.VMEM((tiles, 2, 2, 2, 7, LANES), F32),
             pltpu.SemaphoreType.DMA((tiles,)),
-            pltpu.SemaphoreType.DMA((2, tiles)),
-            pltpu.SemaphoreType.DMA((tiles, 8)),
-            pltpu.SemaphoreType.DMA((tiles, 8)),
+            pltpu.SemaphoreType.DMA((7,)),
+            pltpu.SemaphoreType.DMA((tiles, 14)),
+            pltpu.SemaphoreType.DMA((tiles, 14)),
         ],
         compiler_params=pltpu.CompilerParams(
             collective_id=0, has_side_effects=True, vmem_limit_bytes=40 * 1024 * 1024
         ),
         name="apply",
-    )(control_values, metric_diag, metric_off, mass_weight, orient, forward, mixed, plain)
+    )(
+        *(
+            pltpu.with_memory_space_constraint(x, pltpu.HBM)
+            for x in (control_values, metric_diag, metric_off, mass_weight, orient, forward, mixed, plain)
+        )
+    )
+    return pl.pallas_call(
+        put,
+        out_shape=(shape, shape),
+        in_specs=[pl.BlockSpec(memory_space=pl.ANY)] * 2,
+        out_specs=(in_hbm, in_hbm),
+        scratch_shapes=[pltpu.SemaphoreType.DMA((2, 7))],
+        compiler_params=pltpu.CompilerParams(vmem_limit_bytes=1024 * 1024),
+        name="put",
+    )(*(pltpu.with_memory_space_constraint(x, pltpu.VMEM) for x in results))
 
 
 def solution(mesh):

time: 43.6 us -> 29.4 us (0.67)
  local copies, waits for them, and re-layouts: 8.54 us -> 0 us
  Pallas kernels: 34.1 us -> 28.7 us
    unnamed x18 -> x0, local copies, waits for them, and re-layouts: 8.54 us -> none
    pallas_call x1, Pallas kernels: 34.1 us -> 27.4 us  [per_device(): pl.pallas_call(functools.partial(kernel, values, slopes, tiles), out_shap...]
    pallas_call x0 -> x1, Pallas kernels: none -> 1.26 us  [per_device(): pl.pallas_call(put, out_shape=(shape, shape), in_specs=[pl.BlockSpec(memo...]
where the time goes in v1:
time: 29.4 us; the launch traced here: 29.3 us
  Pallas kernels  28.7 us (98%)
  between operations  0.64 us (2%)
    pallas_call x1, Pallas kernels, per_device(): pl.pallas_call(functools.partial(kernel, values, slopes, tiles), out_shap...  27.4 us
    pallas_call x1, Pallas kernels, per_device(): pl.pallas_call(put, out_shape=(shape, shape), in_specs=[pl.BlockSpec(memo...  1.26 us

profile of v1, /device:TPU:1, one launch (start us, length us, event | category | flops | bytes accessed | tf_op | source)
XLA Modules:
  0.0 29.3 jit_solution(10030612644864270423)
XLA Ops:
  0.6 27.4 %apply.1 = (f32[7,7,7,512]{3,2,1,0:T(8,128)S(1)}, f32[7,7,7,512]{3,2,1,0:T(8,128)S(1)}) custom-call(f32[7,7,7,512]{3,2,1,0:T(8,128)} %control.1, f32[3,8,64]{2,1,0:T(8,128)} %diag_in.1, f32[3,8,64]{2,1,0:T(8,128)} %off_in.1, f32[8,64]{1,0:T(8,128)} %weight_in.1, s32[1,1,1,3]{3,2,1,0:T(1,128)} %orient_in.1, bf16[192,192]{1,0:T(8,128)(2,1)} %constant.6.clone.forward_in, ...), custom_call_target="tpu_custom_call" | custom-call | tf_op jit(solution)/shard_map/apply/pallas_call | solution.py:447
  28.1 1.3 %put.1 = (f32[7,7,7,512]{3,2,1,0:T(8,128)}, f32[7,7,7,512]{3,2,1,0:T(8,128)}) custom-call(f32[7,7,7,512]{3,2,1,0:T(8,128)S(1)} %get-tuple-element.4.stiff, f32[7,7,7,512]{3,2,1,0:T(8,128)S(1)} %get-tuple-element.5.mass), custom_call_target="tpu_custom_call" | custom-call | tf_op jit(solution)/shard_map/put/pallas_call | solution.py:490

commit v2 on v1

--- a/solution.py
+++ b/solution.py
@@ -117,11 +117,11 @@
     values, slopes, tiles,
     control, diag_in, off_in, weight_in, orient_in, forward_in, mixed_in_hbm, plain_in_hbm,
     stiff_out, mass_out,
-    diag, off, weight, orient, forward, mixed, plain,
+    raw, orient, forward, mixed, plain,
     ubuf, gbuf, planes, metric, scales,
     xrecv, ysend_inner, yrecv_inner, ysend_ends, yrecv_ends, yrecv_sides,
     zsend_inner, zrecv_inner, zsend_sides, zrecv_sides,
-    load_sem, small_sem, send_sem, recv_sem,
+    load_sem, small_sem, sems,
 ):
     px, py, pz = (lax.axis_index(a) for a in ("px", "py", "pz"))
     nx, ny, nz = (lax.axis_size(a) for a in ("px", "py", "pz"))
@@ -132,6 +132,31 @@
     odd = lax.rem(px, 2)
     rim = 6 * odd
 
+    def load(t):
+        return pltpu.make_async_copy(
+            control.at[:, :, :, pl.ds(pl.multiple_of(t * LANES, LANES), LANES)],
+            ubuf.at[t, :, :, pl.ds(0, 7), :],
+            load_sem.at[t],
+        )
+
+    small = [
+        pltpu.make_async_copy(source, target, small_sem.at[n])
+        for n, source, target in (
+            (0, orient_in, orient),
+            (1, diag_in, raw.at[pl.ds(0, 3)]),
+            (1, off_in, raw.at[pl.ds(3, 3)]),
+            (1, weight_in, raw.at[6]),
+            (2, forward_in, forward),
+            (3, mixed_in_hbm, mixed),
+            (4, plain_in_hbm, plain),
+        )
+    ]
+    load(0).start()
+    for c in small:
+        c.start()
+    for t in range(1, tiles):
+        load(t).start()
+
     barrier = pltpu.get_barrier_semaphore()
     for device in (
         (x_up, py, pz), (x_down, py, pz),
@@ -140,50 +165,26 @@
     ):
         pl.semaphore_signal(barrier, inc=1, device_id=device, device_id_type=MESH)
 
-    def load(t):
-        return pltpu.make_async_copy(
-            control.at[:, :, :, pl.ds(pl.multiple_of(t * LANES, LANES), LANES)],
-            ubuf.at[t, :, :, pl.ds(0, 7), :],
-            load_sem.at[t],
-        )
-
-    small = [
-        pltpu.make_async_copy(src, dst, small_sem.at[n])
-        for n, (src, dst) in enumerate(
-            (
-                (orient_in, orient), (diag_in, diag), (off_in, off), (weight_in, weight),
-                (forward_in, forward), (mixed_in_hbm, mixed), (plain_in_hbm, plain),
-            )
-        )
-    ]
-    for c in small[:4]:
-        c.start()
-    load(0).start()
-    for c in small[4:]:
-        c.start()
-    for t in range(1, tiles):
-        load(t).start()
     pad = jnp.zeros((7, 7, 1, LANES), F32)
     for t in range(tiles):
         ubuf[t, :, :, pl.ds(7, 1), :] = pad
 
-    for c in small[:4]:
-        c.wait()
+    small[0].wait()
+    pltpu.make_async_copy(raw, raw, small_sem.at[1]).wait()
     flip_i, flip_j, flip_k = (orient[0, 0, 0, d] for d in range(3))
     variant = 2 * flip_j + flip_k
 
-    scales[pl.ds(0, 24), pl.ds(0, 64)] = diag[...].reshape(24, 64)
-    scales[pl.ds(24, 24), pl.ds(0, 64)] = off[...].reshape(24, 64)
-    scales[pl.ds(48, 8), pl.ds(0, 64)] = weight[...]
-    turned = scales[...].T
-    for m in range(56):
-        metric[m] = jnp.broadcast_to(turned[:64, m : m + 1], (64, LANES))
-
-    for c in small[4:]:
-        c.wait()
-
-    def compute(t):
+    scales[pl.ds(0, 56), pl.ds(0, 64)] = raw[...].reshape(56, 64)
+    turned = scales[...].T[:64]
+
+    def spread(m):
+        metric[m] = jnp.broadcast_to(turned[:, m : m + 1], (64, LANES))
+
+    def compute(t, first=False):
         load(t).wait()
+        if first:
+            for c in small[4:]:
+                c.wait()
         forward_table = forward[...]
         mixed_table = mixed[variant]
         plain_table = plain[variant]
@@ -205,6 +206,10 @@
             return at_values, at_slopes
 
         def back(e, at_values, at_slopes):
+            if first:
+                for m in range(7):
+                    spread(8 * m + 2 * e)
+                    spread(8 * m + 2 * e + 1)
             mixed_in, plain_in = [], []
             for n, a in enumerate((2 * e, 2 * e + 1)):
                 lanes = slice(n * LANES, (n + 1) * LANES)
@@ -266,7 +271,7 @@
 
     def remote(t, which, src, dst, device):
         return pltpu.make_async_remote_copy(
-            src_ref=src, dst_ref=dst, send_sem=send_sem.at[t, which], recv_sem=recv_sem.at[t, which],
+            src_ref=src, dst_ref=dst, send_sem=sems.at[t, which], recv_sem=sems.at[t, which],
             device_id=device, device_id_type=MESH,
         )
 
@@ -275,50 +280,57 @@
     def x_copies(t):
         return [
             remote(t, 0, gbuf.at[:, t, 6, :, rows, :], xrecv.at[t, 0, :, :, rows, :], (x_up, py, pz)),
-            remote(t, 1, gbuf.at[:, t, 0, :, rows, :], xrecv.at[t, 1, :, :, rows, :], (x_down, py, pz)),
+            remote(t, 0, gbuf.at[:, t, 0, :, rows, :], xrecv.at[t, 1, :, :, rows, :], (x_down, py, pz)),
         ]
 
     def y_pair(t, which, sent, received):
         return [
             remote(t, which, sent.at[t, 1], received.at[t, 0], (px, y_up, pz)),
-            remote(t, which + 1, sent.at[t, 0], received.at[t, 1], (px, y_down, pz)),
+            remote(t, which, sent.at[t, 0], received.at[t, 1], (px, y_down, pz)),
         ]
 
     def y_inner(t):
-        return y_pair(t, 2, ysend_inner, yrecv_inner)
+        return y_pair(t, 1, ysend_inner, yrecv_inner)
 
     def y_ends(t):
-        return y_pair(t, 4, ysend_ends, yrecv_ends)
+        return y_pair(t, 2, ysend_ends, yrecv_ends)
 
     def y_sides(t):
         near = 6 - rim
         there = 1 - odd
         return [
-            remote(t, 6, gbuf.at[:, t, near, 6, rows, :], yrecv_sides.at[t, 0, there, :, rows, :], (px, y_up, pz)),
-            remote(t, 7, gbuf.at[:, t, near, 0, rows, :], yrecv_sides.at[t, 1, there, :, rows, :], (px, y_down, pz)),
-            remote(t, 8, gbuf.at[:, t, rim, 6, rows, :], yrecv_sides.at[t, 0, there, :, rows, :], (x_mirror, y_up, pz)),
-            remote(t, 9, gbuf.at[:, t, rim, 0, rows, :], yrecv_sides.at[t, 1, there, :, rows, :], (x_mirror, y_down, pz)),
+            remote(t, 3, gbuf.at[:, t, near, 6, rows, :], yrecv_sides.at[t, 0, there, :, rows, :], (px, y_up, pz)),
+            remote(t, 3, gbuf.at[:, t, near, 0, rows, :], yrecv_sides.at[t, 1, there, :, rows, :], (px, y_down, pz)),
+            remote(t, 3, gbuf.at[:, t, rim, 6, rows, :], yrecv_sides.at[t, 0, there, :, rows, :], (x_mirror, y_up, pz)),
+            remote(t, 3, gbuf.at[:, t, rim, 0, rows, :], yrecv_sides.at[t, 1, there, :, rows, :], (x_mirror, y_down, pz)),
         ]
 
     def z_pair(t, which, sent, received):
         return [
             remote(t, which, sent.at[t, 1], received.at[t, 0], (px, py, z_up)),
-            remote(t, which + 1, sent.at[t, 0], received.at[t, 1], (px, py, z_down)),
+            remote(t, which, sent.at[t, 0], received.at[t, 1], (px, py, z_down)),
         ]
 
     def z_inner(t):
-        return z_pair(t, 10, zsend_inner, zrecv_inner)
+        return z_pair(t, 4, zsend_inner, zrecv_inner)
 
     def z_sides(t):
-        return z_pair(t, 12, zsend_sides, zrecv_sides)
+        return z_pair(t, 5, zsend_sides, zrecv_sides)
 
     def start(copies):
         for c in copies:
             c.start()
 
-    def wait(copies):
-        for c in copies:
-            c.wait()
+    def wait(t, which):
+        views = (
+            xrecv.at[pl.ds(0, 2), :, :, :, rows, :],
+            yrecv_inner.at[pl.ds(0, 2)],
+            yrecv_ends.at[pl.ds(0, 2)],
+            yrecv_sides.at[pl.ds(0, 2), :, :, :, rows, :],
+            zrecv_inner.at[pl.ds(0, 2)],
+            zrecv_sides.at[pl.ds(0, 2)],
+        )
+        pltpu.make_async_copy(views[which], views[which], sems.at[t, which]).wait()
 
     def fold_x(t):
         for side in range(2):
@@ -376,50 +388,47 @@
                     tile = gbuf[o, t, i + flip_i * (6 - 2 * i), j + flip_j * (6 - 2 * j)]
                     out[i, j, :, lanes] = jnp.take_along_axis(tile, pick, axis=0)[:7]
 
-    def produce(t, carry):
-        compute(t)
-
-        @pl.when(t == 0)
-        def _():
-            pl.semaphore_wait(barrier, 8)
-
+    def send_first(t):
         start(x_copies(t))
         take_z(t, zsend_inner, inner_rows)
         start(z_inner(t))
         take_y_inner(t)
 
-        @pl.when(t >= 1)
-        def _():
-            start(y_inner(t - 1))
-
+    def produce(t, carry):
+        compute(t)
+        send_first(t)
+        start(y_inner(t - 1))
         return carry
 
     def after_x(t, carry):
-        wait(x_copies(t))
+        wait(t, 0)
         fold_x(t)
         take_z(t, zsend_sides, side_rows)
         start(z_sides(t))
         return carry
 
     def after_z(t, carry):
-        wait(z_inner(t))
+        wait(t, 4)
         fold_z(t, zrecv_inner, inner_rows)
         take_y_ends(t)
         start(y_ends(t))
-        wait(z_sides(t))
+        wait(t, 5)
         fold_z(t, zrecv_sides, side_rows)
         start(y_sides(t))
         return carry
 
     def after_y(t, carry):
-        wait(y_inner(t))
-        wait(y_ends(t))
-        wait(y_sides(t))
+        wait(t, 1)
+        wait(t, 2)
+        wait(t, 3)
         fold_y(t)
         finish(t)
         return carry
 
-    lax.fori_loop(0, tiles, produce, 0)
+    compute(0, first=True)
+    pl.semaphore_wait(barrier, 8)
+    send_first(0)
+    lax.fori_loop(1, tiles, produce, 0)
     start(y_inner(tiles - 1))
     for stage in (after_x, after_z, after_y):
         lax.fori_loop(0, tiles, stage, 0)
@@ -427,8 +436,7 @@
 
 def put(stiff, mass, stiff_out, mass_out, sem):
     copies = [
-        pltpu.make_async_copy(source.at[i], target.at[i], sem.at[n, i])
-        for i in range(7)
+        pltpu.make_async_copy(source, target, sem.at[n])
         for n, (source, target) in enumerate(((stiff, stiff_out), (mass, mass_out)))
     ]
     for c in copies:
@@ -450,9 +458,7 @@
         in_specs=[in_hbm] * 8,
         out_specs=(in_vmem, in_vmem),
         scratch_shapes=[
-            pltpu.VMEM(metric_diag.shape, F32),
-            pltpu.VMEM(metric_off.shape, F32),
-            pltpu.VMEM(mass_weight.shape, F32),
+            pltpu.VMEM((7, 8, 64), F32),
             pltpu.SMEM(orient.shape, jnp.int32),
             pltpu.VMEM(forward.shape, BF16),
             pltpu.VMEM(mixed.shape, BF16),
@@ -473,9 +479,8 @@
             pltpu.VMEM((tiles, 2, 2, 2, 7, LANES), F32),
             pltpu.VMEM((tiles, 2, 2, 2, 7, LANES), F32),
             pltpu.SemaphoreType.DMA((tiles,)),
-            pltpu.SemaphoreType.DMA((7,)),
-            pltpu.SemaphoreType.DMA((tiles, 14)),
-            pltpu.SemaphoreType.DMA((tiles, 14)),
+            pltpu.SemaphoreType.DMA((5,)),
+            pltpu.SemaphoreType.DMA((tiles, 6)),
         ],
         compiler_params=pltpu.CompilerParams(
             collective_id=0, has_side_effects=True, vmem_limit_bytes=40 * 1024 * 1024
@@ -492,7 +497,7 @@
         out_shape=(shape, shape),
         in_specs=[pl.BlockSpec(memory_space=pl.ANY)] * 2,
         out_specs=(in_hbm, in_hbm),
-        scratch_shapes=[pltpu.SemaphoreType.DMA((2, 7))],
+        scratch_shapes=[pltpu.SemaphoreType.DMA((2,))],
         compiler_params=pltpu.CompilerParams(vmem_limit_bytes=1024 * 1024),
         name="put",
     )(*(pltpu.with_memory_space_constraint(x, pltpu.VMEM) for x in results))

time: 29.4 us -> 28.4 us (0.966)
  Pallas kernels: 28.7 us -> 27.6 us
    pallas_call x1, Pallas kernels: 27.4 us -> 26.4 us  [per_device(): pl.pallas_call(functools.partial(kernel, values, slopes, tiles), out_shap...]
where the time goes in v2:
time: 28.4 us; the launch traced here: 28.2 us
  Pallas kernels  27.6 us (97%)
  between operations  0.64 us (2%)
    pallas_call x1, Pallas kernels, per_device(): pl.pallas_call(functools.partial(kernel, values, slopes, tiles), out_shap...  26.4 us
    pallas_call x1, Pallas kernels, per_device(): pl.pallas_call(put, out_shape=(shape, shape), in_specs=[pl.BlockSpec(memo...  1.17 us

profile of v2, /device:TPU:1, one launch (start us, length us, event | category | flops | bytes accessed | tf_op | source)
XLA Modules:
  0.0 28.2 jit_solution(8171625083435684128)
XLA Ops:
  0.6 26.4 %apply.1 = (f32[7,7,7,512]{3,2,1,0:T(8,128)S(1)}, f32[7,7,7,512]{3,2,1,0:T(8,128)S(1)}) custom-call(f32[7,7,7,512]{3,2,1,0:T(8,128)} %control.1, f32[3,8,64]{2,1,0:T(8,128)} %diag_in.1, f32[3,8,64]{2,1,0:T(8,128)} %off_in.1, f32[8,64]{1,0:T(8,128)} %weight_in.1, s32[1,1,1,3]{3,2,1,0:T(1,128)} %orient_in.1, bf16[192,192]{1,0:T(8,128)(2,1)} %constant.6.clone.forward_in, ...), custom_call_target="tpu_custom_call" | custom-call | tf_op jit(solution)/shard_map/apply/pallas_call | solution.py:455
  27.1 1.2 %put.1 = (f32[7,7,7,512]{3,2,1,0:T(8,128)}, f32[7,7,7,512]{3,2,1,0:T(8,128)}) custom-call(f32[7,7,7,512]{3,2,1,0:T(8,128)S(1)} %get-tuple-element.4.stiff, f32[7,7,7,512]{3,2,1,0:T(8,128)S(1)} %get-tuple-element.5.mass), custom_call_target="tpu_custom_call" | custom-call | tf_op jit(solution)/shard_map/put/pallas_call | solution.py:495

commit v3 on v2

--- a/solution.py
+++ b/solution.py
@@ -11,6 +11,7 @@
 
 MESH = pl.DeviceIdType.MESH
 LANES = 128
+LAG = 2
 F32 = jnp.float32
 BF16 = jnp.bfloat16
 
@@ -62,10 +63,8 @@
     return np.einsum("bj,ck->bcjk", wide_first, wide_second).reshape(64, 64)
 
 
-def mirrored(table, flip_j, flip_k):
+def mirrored(table, flip_k):
     grid = table.reshape(64, 8, 8).copy()
-    if flip_j:
-        grid[:, :7] = grid[:, 6::-1]
     if flip_k:
         grid[:, :, :7] = grid[:, :, 6::-1]
     return grid.reshape(64, 64)
@@ -78,9 +77,9 @@
     high, low = split(np.concatenate([value_value, slope_value, value_slope]))
     forward = np.concatenate([high, low, high], axis=1)
     back_mixed, back_plain = [], []
-    for flips in range(4):
+    for flip_k in range(2):
         vv, sv, vs = (
-            split(mirrored(t, flips // 2, flips % 2).T) for t in (value_value, slope_value, value_slope)
+            split(mirrored(t, flip_k).T) for t in (value_value, slope_value, value_slope)
         )
         none = np.zeros((64, 64), vv[0].dtype)
         mixed = np.concatenate([sv[0], vs[0]], axis=1)
@@ -119,7 +118,8 @@
     stiff_out, mass_out,
     raw, orient, forward, mixed, plain,
     ubuf, gbuf, planes, metric, scales,
-    xrecv, ysend_inner, yrecv_inner, ysend_ends, yrecv_ends, yrecv_sides,
+    xrecv, ysend_inner, yrecv_inner, ysend_ends, yrecv_ends,
+    ysend_sides, yrecv_sides, ysend_corners, yrecv_corners,
     zsend_inner, zrecv_inner, zsend_sides, zrecv_sides,
     load_sem, small_sem, sems,
 ):
@@ -130,7 +130,14 @@
     z_up, z_down = lax.rem(pz + 1, nz), lax.rem(pz + nz - 1, nz)
     x_mirror = nx - 1 - px
     odd = lax.rem(px, 2)
-    rim = 6 * odd
+
+    barrier = pltpu.get_barrier_semaphore()
+    for device in (
+        (x_up, py, pz), (x_down, py, pz),
+        (px, y_up, pz), (px, y_down, pz), (x_mirror, y_up, pz), (x_mirror, y_down, pz),
+        (px, py, z_up), (px, py, z_down),
+    ):
+        pl.semaphore_signal(barrier, inc=1, device_id=device, device_id_type=MESH)
 
     def load(t):
         return pltpu.make_async_copy(
@@ -157,14 +164,6 @@
     for t in range(1, tiles):
         load(t).start()
 
-    barrier = pltpu.get_barrier_semaphore()
-    for device in (
-        (x_up, py, pz), (x_down, py, pz),
-        (px, y_up, pz), (px, y_down, pz), (x_mirror, y_up, pz), (x_mirror, y_down, pz),
-        (px, py, z_up), (px, py, z_down),
-    ):
-        pl.semaphore_signal(barrier, inc=1, device_id=device, device_id_type=MESH)
-
     pad = jnp.zeros((7, 7, 1, LANES), F32)
     for t in range(tiles):
         ubuf[t, :, :, pl.ds(7, 1), :] = pad
@@ -172,7 +171,6 @@
     small[0].wait()
     pltpu.make_async_copy(raw, raw, small_sem.at[1]).wait()
     flip_i, flip_j, flip_k = (orient[0, 0, 0, d] for d in range(3))
-    variant = 2 * flip_j + flip_k
 
     scales[pl.ds(0, 56), pl.ds(0, 64)] = raw[...].reshape(56, 64)
     turned = scales[...].T[:64]
@@ -183,11 +181,8 @@
     def compute(t, first=False):
         load(t).wait()
         if first:
-            for c in small[4:]:
-                c.wait()
+            small[4].wait()
         forward_table = forward[...]
-        mixed_table = mixed[variant]
-        plain_table = plain[variant]
         nothing = jnp.zeros((8, LANES), F32)
         def ahead(e):
             source = [ubuf[t, i].reshape(56, LANES) for i in range(e, e + 4)]
@@ -251,23 +246,28 @@
                 )
                 mass = mac([(values[2 * e + n, i], terms[n][2]) for n in range(2)])
                 if e > 0 and i < e + 3:
-                    stiff = stiff + planes[0, i]
-                    mass = mass + planes[1, i]
-                planes[0, i] = stiff
-                planes[1, i] = mass
-
-        up = {0: ahead(0), 1: ahead(1)}
+                    stiff = stiff + planes[0, i].reshape(56, LANES)
+                    mass = mass + planes[1, i].reshape(56, LANES)
+                planes[0, i] = stiff.reshape(7, 8, LANES)
+                planes[1, i] = mass.reshape(7, 8, LANES)
+
+        up = {e: ahead(e) for e in range(4)}
+        if first:
+            small[5].wait()
+            small[6].wait()
+        mixed_table = mixed[flip_k]
+        plain_table = plain[flip_k]
         down = {}
         for e in range(4):
             down[e] = back(e, *up.pop(e))
-            if e + 2 < 4:
-                up[e + 2] = ahead(e + 2)
             if e >= 1:
                 gather(e - 1, *down.pop(e - 1))
-        gather(3, *down.pop(3))
+        for e in range(4 - 1, 4):
+            gather(e, *down.pop(e))
         for o in range(2):
             for i in range(7):
-                gbuf[o, t, i] = planes[o, i + flip_i * (6 - 2 * i)].reshape(7, 8, LANES)
+                for j in range(7):
+                    gbuf[o, t, i, j] = planes[o, i + flip_i * (6 - 2 * i), j + flip_j * (6 - 2 * j)]
 
     def remote(t, which, src, dst, device):
         return pltpu.make_async_remote_copy(
@@ -295,15 +295,20 @@
     def y_ends(t):
         return y_pair(t, 2, ysend_ends, yrecv_ends)
 
+    def y_rims(t, which, sent, received):
+        near = 1 - odd
+        return [
+            remote(t, which, sent.at[t, 1, near], received.at[t, 0, near], (px, y_up, pz)),
+            remote(t, which, sent.at[t, 0, near], received.at[t, 1, near], (px, y_down, pz)),
+            remote(t, which, sent.at[t, 1, odd], received.at[t, 0, near], (x_mirror, y_up, pz)),
+            remote(t, which, sent.at[t, 0, odd], received.at[t, 1, near], (x_mirror, y_down, pz)),
+        ]
+
     def y_sides(t):
-        near = 6 - rim
-        there = 1 - odd
-        return [
-            remote(t, 3, gbuf.at[:, t, near, 6, rows, :], yrecv_sides.at[t, 0, there, :, rows, :], (px, y_up, pz)),
-            remote(t, 3, gbuf.at[:, t, near, 0, rows, :], yrecv_sides.at[t, 1, there, :, rows, :], (px, y_down, pz)),
-            remote(t, 3, gbuf.at[:, t, rim, 6, rows, :], yrecv_sides.at[t, 0, there, :, rows, :], (x_mirror, y_up, pz)),
-            remote(t, 3, gbuf.at[:, t, rim, 0, rows, :], yrecv_sides.at[t, 1, there, :, rows, :], (x_mirror, y_down, pz)),
-        ]
+        return y_rims(t, 3, ysend_sides, yrecv_sides)
+
+    def y_corners(t):
+        return y_rims(t, 6, ysend_corners, yrecv_corners)
 
     def z_pair(t, which, sent, received):
         return [
@@ -326,9 +331,10 @@
             xrecv.at[pl.ds(0, 2), :, :, :, rows, :],
             yrecv_inner.at[pl.ds(0, 2)],
             yrecv_ends.at[pl.ds(0, 2)],
-            yrecv_sides.at[pl.ds(0, 2), :, :, :, rows, :],
+            yrecv_sides.at[pl.ds(0, 2)],
             zrecv_inner.at[pl.ds(0, 2)],
             zrecv_sides.at[pl.ds(0, 2)],
+            yrecv_corners.at[pl.ds(0, 2)],
         )
         pltpu.make_async_copy(views[which], views[which], sems.at[t, which]).wait()
 
@@ -366,6 +372,19 @@
             for o in range(2):
                 for n in range(2):
                     ysend_ends[t, side, o, n] = gbuf[o, t, mid, 6 * side, 6 * n, :]
+
+    def take_y_sides(t):
+        for side in range(2):
+            for o in range(2):
+                for n in range(2):
+                    ysend_sides[t, side, n, o] = gbuf[o, t, 6 * n, 6 * side, mid, :]
+
+    def take_y_corners(t):
+        for side in range(2):
+            for o in range(2):
+                for n in range(2):
+                    for m in range(2):
+                        ysend_corners[t, side, n, o, m] = gbuf[o, t, 6 * n, 6 * side, 6 * m, :]
 
     def fold_y(t):
         for side in range(2):
@@ -374,19 +393,27 @@
                 gbuf[o, t, mid, j, mid, :] = gbuf[o, t, mid, j, mid, :] + yrecv_inner[t, side, o]
                 for n in range(2):
                     gbuf[o, t, mid, j, 6 * n, :] = gbuf[o, t, mid, j, 6 * n, :] + yrecv_ends[t, side, o, n]
-                    gbuf[o, t, 6 * n, j, rows, :] = gbuf[o, t, 6 * n, j, rows, :] + yrecv_sides[t, side, n, o, rows, :]
+                    gbuf[o, t, 6 * n, j, mid, :] = gbuf[o, t, 6 * n, j, mid, :] + yrecv_sides[t, side, n, o]
+
+    def fold_corners(t):
+        for side in range(2):
+            for o in range(2):
+                for n in range(2):
+                    for m in range(2):
+                        gbuf[o, t, 6 * n, 6 * side, 6 * m, :] = (
+                            gbuf[o, t, 6 * n, 6 * side, 6 * m, :] + yrecv_corners[t, side, n, o, m]
+                        )
 
     sublane = lax.broadcasted_iota(jnp.int32, (8, LANES), 0)
     turned_rows = jnp.where(sublane < 7, 6 - sublane, sublane)
     pick = sublane + flip_k * (turned_rows - sublane)
 
-    def finish(t):
+    def finish(t, where):
         lanes = pl.ds(pl.multiple_of(t * LANES, LANES), LANES)
         for o, out in enumerate((stiff_out, mass_out)):
-            for i in range(7):
-                for j in range(7):
-                    tile = gbuf[o, t, i + flip_i * (6 - 2 * i), j + flip_j * (6 - 2 * j)]
-                    out[i, j, :, lanes] = jnp.take_along_axis(tile, pick, axis=0)[:7]
+            for i, j in where:
+                tile = gbuf[o, t, i + flip_i * (6 - 2 * i), j + flip_j * (6 - 2 * j)]
+                out[i, j, :, lanes] = jnp.take_along_axis(tile, pick, axis=0)[:7]
 
     def send_first(t):
         start(x_copies(t))
@@ -400,29 +427,56 @@
         start(y_inner(t - 1))
         return carry
 
-    def after_x(t, carry):
+    def after_x(t):
+        wait(t, 4)
+        fold_z(t, zrecv_inner, inner_rows)
+        take_y_ends(t)
+        start(y_ends(t))
         wait(t, 0)
         fold_x(t)
         take_z(t, zsend_sides, side_rows)
         start(z_sides(t))
-        return carry
-
-    def after_z(t, carry):
-        wait(t, 4)
-        fold_z(t, zrecv_inner, inner_rows)
-        take_y_ends(t)
-        start(y_ends(t))
+        take_y_sides(t)
+        start(y_sides(t))
+
+    def after_z(t):
         wait(t, 5)
         fold_z(t, zrecv_sides, side_rows)
-        start(y_sides(t))
+        take_y_corners(t)
+        start(y_corners(t))
+
+    def exchange(t, carry):
+        after_x(t)
+
+        @pl.when(t >= LAG)
+        def _():
+            after_z(t - LAG)
+
         return carry
 
+    def rest(t, carry):
+        after_z(t)
+        return carry
+
+    between = [(i, j) for i in range(7) for j in range(1, 6)]
+    faces = [(i, j) for i in range(1, 6) for j in (0, 6)]
+    corners = [(i, j) for i in (0, 6) for j in (0, 6)]
+
+    def close(t, carry):
+        finish(t, between)
+        return carry
+
     def after_y(t, carry):
-        wait(t, 1)
-        wait(t, 2)
-        wait(t, 3)
+        for which in (1, 2, 3):
+            wait(t, which)
         fold_y(t)
-        finish(t)
+        finish(t, faces)
+        return carry
+
+    def after_corners(t, carry):
+        wait(t, 6)
+        fold_corners(t)
+        finish(t, corners)
         return carry
 
     compute(0, first=True)
@@ -430,7 +484,9 @@
     send_first(0)
     lax.fori_loop(1, tiles, produce, 0)
     start(y_inner(tiles - 1))
-    for stage in (after_x, after_z, after_y):
+    lax.fori_loop(0, tiles, exchange, 0)
+    lax.fori_loop(tiles - LAG, tiles, rest, 0)
+    for stage in (close, after_y, after_corners):
         lax.fori_loop(0, tiles, stage, 0)
 
 
@@ -465,7 +521,7 @@
             pltpu.VMEM(plain.shape, BF16),
             pltpu.VMEM((tiles, 7, 7, 8, LANES), F32),
             pltpu.VMEM((2, tiles, 7, 7, 8, LANES), F32),
-            pltpu.VMEM((2, 7, 56, LANES), F32),
+            pltpu.VMEM((2, 7, 7, 8, LANES), F32),
             pltpu.VMEM((56, 64, LANES), F32),
             pltpu.VMEM((128, 128), F32),
             pltpu.VMEM((tiles, 2, 2, 7, 8, LANES), F32),
@@ -473,14 +529,17 @@
             pltpu.VMEM((tiles, 2, 2, 5, 5, LANES), F32),
             pltpu.VMEM((tiles, 2, 2, 2, 5, LANES), F32),
             pltpu.VMEM((tiles, 2, 2, 2, 5, LANES), F32),
-            pltpu.VMEM((tiles, 2, 2, 2, 8, LANES), F32),
+            pltpu.VMEM((tiles, 2, 2, 2, 5, LANES), F32),
+            pltpu.VMEM((tiles, 2, 2, 2, 5, LANES), F32),
+            pltpu.VMEM((tiles, 2, 2, 2, 2, LANES), F32),
+            pltpu.VMEM((tiles, 2, 2, 2, 2, LANES), F32),
             pltpu.VMEM((tiles, 2, 2, 5, 7, LANES), F32),
             pltpu.VMEM((tiles, 2, 2, 5, 7, LANES), F32),
             pltpu.VMEM((tiles, 2, 2, 2, 7, LANES), F32),
             pltpu.VMEM((tiles, 2, 2, 2, 7, LANES), F32),
             pltpu.SemaphoreType.DMA((tiles,)),
             pltpu.SemaphoreType.DMA((5,)),
-            pltpu.SemaphoreType.DMA((tiles, 6)),
+            pltpu.SemaphoreType.DMA((tiles, 7)),
         ],
         compiler_params=pltpu.CompilerParams(
             collective_id=0, has_side_effects=True, vmem_limit_bytes=40 * 1024 * 1024

time: 28.4 us -> 28.4 us (level)
  no operation moved by 1% of the time
where the time goes in v3:
time: 28.4 us; the launch traced here: 28.3 us
  Pallas kernels  27.7 us (98%)
  between operations  0.64 us (2%)
    pallas_call x1, Pallas kernels, per_device(): pl.pallas_call(functools.partial(kernel, values, slopes, tiles), out_shap...  26.5 us
    pallas_call x1, Pallas kernels, per_device(): pl.pallas_call(put, out_shape=(shape, shape), in_specs=[pl.BlockSpec(memo...  1.17 us

profile of v3, /device:TPU:1, one launch (start us, length us, event | category | flops | bytes accessed | tf_op | source)
XLA Modules:
  0.0 28.3 jit_solution(13238123888872440962)
XLA Ops:
  0.6 26.5 %apply.1 = (f32[7,7,7,512]{3,2,1,0:T(8,128)S(1)}, f32[7,7,7,512]{3,2,1,0:T(8,128)S(1)}) custom-call(f32[7,7,7,512]{3,2,1,0:T(8,128)} %control.1, f32[3,8,64]{2,1,0:T(8,128)} %diag_in.1, f32[3,8,64]{2,1,0:T(8,128)} %off_in.1, f32[8,64]{1,0:T(8,128)} %weight_in.1, s32[1,1,1,3]{3,2,1,0:T(1,128)} %orient_in.1, bf16[192,192]{1,0:T(8,128)(2,1)} %constant.6.clone.forward_in, ...), custom_call_target="tpu_custom_call" | custom-call | tf_op jit(solution)/shard_map/apply/pallas_call | solution.py:511
  27.1 1.2 %put.1 = (f32[7,7,7,512]{3,2,1,0:T(8,128)}, f32[7,7,7,512]{3,2,1,0:T(8,128)}) custom-call(f32[7,7,7,512]{3,2,1,0:T(8,128)S(1)} %get-tuple-element.4.stiff, f32[7,7,7,512]{3,2,1,0:T(8,128)S(1)} %get-tuple-element.5.mass), custom_call_target="tpu_custom_call" | custom-call | tf_op jit(solution)/shard_map/put/pallas_call | solution.py:554

commit v4 on v2

--- a/solution.py
+++ b/solution.py
@@ -132,6 +132,14 @@
     odd = lax.rem(px, 2)
     rim = 6 * odd
 
+    barrier = pltpu.get_barrier_semaphore()
+    for device in (
+        (x_up, py, pz), (x_down, py, pz),
+        (px, y_up, pz), (px, y_down, pz), (x_mirror, y_up, pz), (x_mirror, y_down, pz),
+        (px, py, z_up), (px, py, z_down),
+    ):
+        pl.semaphore_signal(barrier, inc=1, device_id=device, device_id_type=MESH)
+
     def load(t):
         return pltpu.make_async_copy(
             control.at[:, :, :, pl.ds(pl.multiple_of(t * LANES, LANES), LANES)],
@@ -156,14 +164,6 @@
         c.start()
     for t in range(1, tiles):
         load(t).start()
-
-    barrier = pltpu.get_barrier_semaphore()
-    for device in (
-        (x_up, py, pz), (x_down, py, pz),
-        (px, y_up, pz), (px, y_down, pz), (x_mirror, y_up, pz), (x_mirror, y_down, pz),
-        (px, py, z_up), (px, py, z_down),
-    ):
-        pl.semaphore_signal(barrier, inc=1, device_id=device, device_id_type=MESH)
 
     pad = jnp.zeros((7, 7, 1, LANES), F32)
     for t in range(tiles):
@@ -256,12 +256,10 @@
                 planes[0, i] = stiff
                 planes[1, i] = mass
 
-        up = {0: ahead(0), 1: ahead(1)}
+        up = {e: ahead(e) for e in range(4)}
         down = {}
         for e in range(4):
             down[e] = back(e, *up.pop(e))
-            if e + 2 < 4:
-                up[e + 2] = ahead(e + 2)
             if e >= 1:
                 gather(e - 1, *down.pop(e - 1))
         gather(3, *down.pop(3))

time: 28.4 us -> 28.6 us (level)
  no operation moved by 1% of the time
where the time goes in v4:
time: 28.6 us; the launch traced here: 28.4 us
  Pallas kernels  27.7 us (97%)
  between operations  0.64 us (2%)
    pallas_call x1, Pallas kernels, per_device(): pl.pallas_call(functools.partial(kernel, values, slopes, tiles), out_shap...  26.6 us
    pallas_call x1, Pallas kernels, per_device(): pl.pallas_call(put, out_shape=(shape, shape), in_specs=[pl.BlockSpec(memo...  1.17 us

profile of v4, /device:TPU:1, one launch (start us, length us, event | category | flops | bytes accessed | tf_op | source)
XLA Modules:
  0.0 28.4 jit_solution(16275008755209233827)
XLA Ops:
  0.6 26.6 %apply.1 = (f32[7,7,7,512]{3,2,1,0:T(8,128)S(1)}, f32[7,7,7,512]{3,2,1,0:T(8,128)S(1)}) custom-call(f32[7,7,7,512]{3,2,1,0:T(8,128)} %control.1, f32[3,8,64]{2,1,0:T(8,128)} %diag_in.1, f32[3,8,64]{2,1,0:T(8,128)} %off_in.1, f32[8,64]{1,0:T(8,128)} %weight_in.1, s32[1,1,1,3]{3,2,1,0:T(1,128)} %orient_in.1, bf16[192,192]{1,0:T(8,128)(2,1)} %constant.6.clone.forward_in, ...), custom_call_target="tpu_custom_call" | custom-call | tf_op jit(solution)/shard_map/apply/pallas_call | solution.py:453
  27.2 1.2 %put.1 = (f32[7,7,7,512]{3,2,1,0:T(8,128)}, f32[7,7,7,512]{3,2,1,0:T(8,128)}) custom-call(f32[7,7,7,512]{3,2,1,0:T(8,128)S(1)} %get-tuple-element.4.stiff, f32[7,7,7,512]{3,2,1,0:T(8,128)S(1)} %get-tuple-element.5.mass), custom_call_target="tpu_custom_call" | custom-call | tf_op jit(solution)/shard_map/put/pallas_call | solution.py:493
